TPU v7x, 32 devices: a whole 2x2x4 slice. The times are simulated.
32 devices in a mesh: expert: 8 (over z, y), vocab: 4 (over x, core).
Axes of the slice: x: 2, y: 2, z: 4, core: 2. Of those that a mesh axis runs over, the one named last changes fastest.
Arguments:
- layer_out: bfloat16 [256, 2048], P('expert'), may hold values from -6 to 6
- moe_input: bfloat16 [256, 2048], P('expert'), may hold values from -6 to 6
- final_gain: float32 [2048], replicated, may hold values from 0.1 to 1.9
- head_weight: bfloat16 [2048, 12288], P(None, ('expert', 'vocab')), may hold values from -0.125 to 0.125
- clean_ids: int32 [256], P('expert'), may hold values from 0 to 12287
- levels: int32 [256], P('expert'), may hold values from 0 to 15
- ratio_table: float32 [16], replicated, may hold values from 0.5 to 8
- gate_weights: float32 [256, 8], P('expert'), may hold values from 0.05 to 0.5
- expert_ids: int32 [256, 8], P('expert'), may hold values from 0 to 15, all different within a row; in each aligned block of 32 rows (0 to 31, 32 to 63, ...) at most 32 rows name the same one
- w_gate: bfloat16 [16, 2048, 1024], P('expert', None, 'vocab'), may hold values from -0.125 to 0.125
- w_up: bfloat16 [16, 2048, 1024], P('expert', None, 'vocab'), may hold values from -0.125 to 0.125
- w_down: bfloat16 [16, 1024, 2048], P('expert', 'vocab'), may hold values from -0.1875 to 0.1875
Outputs:
- head_grad: float32 [2048, 12288], P(None, ('expert', 'vocab'))
- residual_grad: float32 [256, 2048], P('expert', 'vocab')
- input_grad: float32 [256, 2048], P('expert', 'vocab')
Inputs may be any that keep to these rules, and one draw needn't show every extreme that they name: `expert_ids`: the 8 experts of a row are distinct; among the 32 rows of one index of expert no expert is named by more than 32 rows.
All inputs are finite; a program needn't handle non-finite values.
Results may differ from a plain program's by a relative error of at most 0.0044.
The roundings to bfloat16 on the way count: a program that leaves them out, or rounds other values in their place, can miss the bound.
Values may be sent and summed in bfloat16 or wider, within the bound.
A program may use at most 64 MiB of HBM per device.

v0:
```python
import math
import jax
import jax.numpy as jnp
from jax import lax
from jax.sharding import PartitionSpec as P

epsilon = 1e-05


def on_device(
    layer_out,
    moe_input,
    final_gain,
    head_weight,
    clean_ids,
    levels,
    ratio_table,
    gate_weights,
    expert_ids,
    w_gate,
    w_up,
    w_down,
):
    rows_local, model_width = layer_out.shape
    top_count = expert_ids.shape[1]
    n_expert = lax.axis_size("expert")
    n_vocab = lax.axis_size("vocab")
    total_rows = rows_local * n_expert
    local_experts = w_gate.shape[0]
    experts_all = local_experts * n_expert
    capacity = max(2, 2 * rows_local * top_count // experts_all)
    feature_share = model_width // n_vocab
    vocab_local = head_weight.shape[1]
    values = layer_out.astype(jnp.float32)
    row_scale = jnp.sqrt(jnp.mean(values * values, axis=1, keepdims=True) + epsilon)
    unit_rows = values / row_scale
    normed = (unit_rows * final_gain[None, :]).astype(jnp.bfloat16)
    normed_all, clean_all, level_all = (
        lax.all_gather(normed, "expert", axis=0, tiled=True),
        lax.all_gather(clean_ids, "expert", axis=0, tiled=True),
        lax.all_gather(levels, "expert", axis=0, tiled=True),
    )
    level_labels = jnp.arange(ratio_table.shape[0], dtype=jnp.int32)
    ratio_rows = jnp.sum(
        jnp.where(level_all[:, None] == level_labels[None, :], ratio_table[None, :], 0.0), axis=1
    )
    column_start = (lax.axis_index("expert") * n_vocab + lax.axis_index("vocab")) * vocab_local
    columns = column_start + jnp.arange(vocab_local, dtype=jnp.int32)
    scores = jnp.dot(normed_all, head_weight, preferred_element_type=jnp.float32)
    target_hit = (clean_all[:, None] == columns[None, :]).astype(jnp.float32)
    loss_scale = 1.0 / math.sqrt(total_rows)
    score_grad = ((jnp.exp(scores) - ratio_rows[:, None] * target_hit) * loss_scale).astype(
        jnp.bfloat16
    )
    head_grad = lax.dot_general(
        normed_all, score_grad, (((0,), (0,)), ((), ())), preferred_element_type=jnp.float32
    )
    partial_grad = lax.psum_scatter(
        lax.dot_general(
            score_grad, head_weight, (((1,), (1,)), ((), ())), preferred_element_type=jnp.float32
        ),
        "expert",
        scatter_dimension=0,
        tiled=True,
    )
    normed_grad = lax.psum(partial_grad, "vocab")
    gained = final_gain[None, :] * normed_grad
    residual_full = (
        gained - unit_rows * jnp.mean(unit_rows * gained, axis=1, keepdims=True)
    ) / row_scale
    feature_start = lax.axis_index("vocab") * feature_share
    residual_grad = lax.dynamic_slice_in_dim(residual_full, feature_start, feature_share, 1)
    flat_ids = expert_ids.reshape(-1)
    labels = jnp.arange(experts_all, dtype=jnp.int32)
    onehot = (flat_ids[:, None] == labels[None, :]).astype(jnp.int32)
    earlier = jnp.cumsum(onehot, axis=0) - onehot
    slot_index = jnp.sum(earlier * onehot, axis=1)
    position = flat_ids * capacity + slot_index
    routed_grad = (
        (gate_weights[:, :, None] * residual_full[:, None, :])
        .astype(jnp.bfloat16)
        .reshape(-1, model_width)
    )
    inputs_rep = jnp.repeat(moe_input, top_count, axis=0)
    buffer_rows = experts_all * capacity
    send_inputs = (
        jnp.zeros((buffer_rows, model_width), jnp.bfloat16)
        .at[position]
        .set(inputs_rep)
        .reshape(experts_all, capacity, model_width)
    )
    send_grads = (
        jnp.zeros((buffer_rows, model_width), jnp.bfloat16)
        .at[position]
        .set(routed_grad)
        .reshape(experts_all, capacity, model_width)
    )
    part_inputs = lax.dynamic_slice_in_dim(send_inputs, feature_start, feature_share, 2)
    part_grads = lax.dynamic_slice_in_dim(send_grads, feature_start, feature_share, 2)
    moved_inputs, moved_grads = (
        lax.all_to_all(part_inputs, "expert", split_axis=0, concat_axis=1, tiled=True),
        lax.all_to_all(part_grads, "expert", split_axis=0, concat_axis=1, tiled=True),
    )
    inputs_slot, grads_slot = (
        lax.all_gather(moved_inputs, "vocab", axis=2, tiled=True),
        lax.all_gather(moved_grads, "vocab", axis=2, tiled=True),
    )
    gate_pre = jnp.einsum("esd,edf->esf", inputs_slot, w_gate, preferred_element_type=jnp.float32)
    up_pre = jnp.einsum("esd,edf->esf", inputs_slot, w_up, preferred_element_type=jnp.float32)
    act_grad = jnp.einsum("esd,efd->esf", grads_slot, w_down, preferred_element_type=jnp.float32)
    sigmoid_gate = jax.nn.sigmoid(gate_pre)
    gate_grad = (act_grad * up_pre * sigmoid_gate * (1.0 + gate_pre * (1.0 - sigmoid_gate))).astype(
        jnp.bfloat16
    )
    up_grad = (act_grad * gate_pre * sigmoid_gate).astype(jnp.bfloat16)
    partial_input = jnp.einsum(
        "esf,edf->esd", gate_grad, w_gate, preferred_element_type=jnp.float32
    )
    partial_input = partial_input + jnp.einsum(
        "esf,edf->esd", up_grad, w_up, preferred_element_type=jnp.float32
    )
    slot_share = lax.psum_scatter(partial_input, "vocab", scatter_dimension=2, tiled=True)
    returned = lax.all_to_all(slot_share, "expert", split_axis=1, concat_axis=0, tiled=True)
    per_pair = returned.reshape(-1, feature_share)[position]
    input_grad = jnp.sum(per_pair.reshape(rows_local, top_count, feature_share), axis=1)
    return (head_grad, residual_grad, input_grad)


def solution(mesh):
    in_specs = (
        P("expert", None),
        P("expert", None),
        P(),
        P(None, ("expert", "vocab")),
        P("expert"),
        P("expert"),
        P(),
        P("expert", None),
        P("expert", None),
        P("expert", None, "vocab"),
        P("expert", None, "vocab"),
        P("expert", "vocab", None),
    )
    out_specs = (P(None, ("expert", "vocab")), P("expert", "vocab"), P("expert", "vocab"))
    return jax.shard_map(
        on_device, mesh=mesh, in_specs=in_specs, out_specs=out_specs, check_vma=False
    )
```

profile of v0, /device:TPU:0, one launch (start us, length us, event | category | flops | bytes accessed | tf_op | source)
XLA Modules:
  0.0 321.3 jit_solution(14341958270852453572)
XLA Ops:
  8.4 1.7 multiply_convert_fusion.2
  13.8 13.1 %all-reduce.2 = (s32[256]{0:T(256)S(1)}, s32[256]{0:T(256)S(1)}) all-reduce(s32[256]{0:T(256)S(1)} %dynamic-update-slice.1, s32[256]{0:T(256)S(1)} %dynamic-update-slice), channel_id=1, replica_groups=mesh['expert'=8,'vocab'=4] {'expert'}, use_global_device_ids=true, to_apply=%add.1 | all-reduce | flops 512 | bytes 4096
  27.7 26.3 %all-gather.4.cloned.1.call-done = bf16[256,2048]{1,0:T(8,128)(2,1)} async-done(((bf16[32,2048]{1,0:T(8,128)(2,1)}), bf16[256,2048]{1,0:T(8,128)(2,1)}) %all-gather.4.cloned.1.call-update) | async-done | bytes 1048592 | tf_op jit(solution)/shard_map/all_gather | solution.py:39
  53.9 2.6 fusion.6
  57.2 2.1 fusion.30
  60.7 3.7 %scatter_custom_fusion.1 = bf16[512,2048]{1,0:T(8,128)(2,1)} fusion(s32[256]{0:T(256)S(1)} %bitcast.68, bf16[]{:T(256)} %constant.39.clone.1, bf16[32,2048]{1,0:T(8,128)(2,1)S(1)} %copy-done.5), kind=kCustom, calls=%fused_computation.16 | custom fusion | bytes 2228226 | tf_op jit(solution)/shard_map/scatter | solution.py:89
  64.4 2.0 constant_dynamic-slice_fusion
  66.4 3.5 %all-to-all-start.1 = ((bf16[16,32,512]{2,1,0:T(8,128)(2,1)}), bf16[16,32,512]{2,1,0:T(8,128)(2,1)S(1)}, u32[]{:S(2)}, u32[]{:S(2)}) async-start(bf16[16,32,512]{2,1,0:T(8,128)(2,1)} %constant_dynamic-slice_fusion), calls=%async_computation.2 | async-start | bytes 1048576 | tf_op jit(solution)/shard_map/all_to_all | solution.py:101
  70.0 64.0 %reduce-scatter.3.cloned.1.call-done = f32[32,2048]{1,0:T(8,128)} async-done(((f32[256,2048]{1,0:T(8,128)}), f32[32,2048]{1,0:T(8,128)}) %reduce-scatter.3.cloned.1.call-update) | async-done | bytes 262160 | tf_op jit(solution)/shard_map/reduce_scatter | solution.py:58
  135.1 32.5 %all-reduce.5.cloned.1.call-done = f32[32,2048]{1,0:T(8,128)} async-done(((f32[32,2048]{1,0:T(8,128)}), f32[32,2048]{1,0:T(8,128)}) %all-reduce.5.cloned.1.call-update) | async-done | bytes 262160 | tf_op jit(solution)/shard_map/psum | solution.py:66
  169.9 3.8 %scatter_custom_fusion = bf16[512,2048]{1,0:T(8,128)(2,1)} fusion(s32[256]{0:T(256)S(1)} %bitcast.69, f32[32,2048]{1,0:T(8,128)S(1)} %subtract_divide_fusion, f32[256]{0:T(256)S(1)} %mul.124, bf16[]{:T(256)} %constant.39.clone.1), kind=kCustom, calls=%fused_computation.15 | custom fusion | flops 1048576 | bytes 2360322 | tf_op jit(solution)/shard_map/scatter | solution.py:95
  174.7 18.6 %all_to_all.51 = bf16[16,32,512]{2,1,0:T(8,128)(2,1)S(1)} all-to-all(bf16[16,32,512]{2,1,0:T(8,128)(2,1)S(1)} %constant_dynamic-slice_fusion.1), channel_id=1, replica_groups=mesh['expert'=8,'vocab'=4] {'expert'}, dimensions={0} | all-to-all | bytes 1048576 | tf_op jit(solution)/shard_map/all_to_all | solution.py:102
  194.5 2.9 fusion.32
  197.4 18.8 %all-gather.6.cloned.1.call-done = bf16[2,256,2048]{2,1,0:T(8,128)(2,1)} async-done(((bf16[2,256,512]{2,1,0:T(8,128)(2,1)}), bf16[2,256,2048]{2,1,0:T(8,128)(2,1)}) %all-gather.6.cloned.1.call-update) | async-done | bytes 2097168 | tf_op jit(solution)/shard_map/all_gather | solution.py:106
  216.2 3.0 fusion.31
  219.2 5.6 %fusion.7 = f32[2,256,2048]{2,1,0:T(8,128)} fusion(bf16[2,2048,256]{2,1,0:T(8,128)(2,1)} %param.21, f32[2,256,256]{2,1,0:T(8,128)S(1)} %fusion.31, bf16[2,256,2048]{2,1,0:T(8,128)(2,1)} %all-gather.8.cloned.1.call-done, bf16[2,2048,256]{2,1,0:T(8,128)(2,1)S(1)} %copy-done, f32[2,256,256]{2,1,0:T(8,128)S(1)} %fusion.32), kind=kOutput, calls=%fused_computation.14 | convolution fusion | flops 1075052544 | bytes 11534336 | tf_op jit(solution)/shard_map/esf,edf->esd/dot_general | solution.py:116
  224.8 4.9 %convolution_add_fusion = f32[2,256,2048]{2,1,0:T(8,128)} fusion(f32[2,256,2048]{2,1,0:T(8,128)} %fusion.7, bf16[2,2048,256]{2,1,0:T(8,128)(2,1)S(1)} %copy-done, f32[2,256,256]{2,1,0:T(8,128)S(1)} %fusion.31, f32[2,256,256]{2,1,0:T(8,128)S(1)} %fusion.32), kind=kOutput, calls=%fused_computation.3 | convolution fusion | flops 538705920 | bytes 11534336 | tf_op jit(solution)/shard_map/esf,edf->esd/dot_general | solution.py:119
  229.7 44.6 %reduce-scatter.5.cloned.1.call-done = f32[2,256,512]{2,1,0:T(8,128)} async-done(((f32[2,256,2048]{2,1,0:T(8,128)}), f32[2,256,512]{2,1,0:T(8,128)}) %reduce-scatter.5.cloned.1.call-update) | async-done | bytes 1048592 | tf_op jit(solution)/shard_map/reduce_scatter | solution.py:122
  274.2 3.0 copy.40
  277.3 5.5 %all-to-all-start.2 = ((f32[2,256,512]{2,0,1:T(2,128)}), f32[2,256,512]{2,0,1:T(2,128)S(1)}, u32[]{:S(2)}, u32[]{:S(2)}) async-start(f32[2,256,512]{2,0,1:T(2,128)} %copy.40), calls=%async_computation.4 | async-start | bytes 2097152 | tf_op jit(solution)/shard_map/all_to_all | solution.py:123
  282.8 3.7 %fusion.29 = f32[2048,384]{1,0:T(8,128)} fusion(bf16[256,2048]{1,0:T(8,128)(2,1)} %all-gather.4.cloned.1.call-done, bf16[256,384]{1,0:T(8,128)(2,1)} %copy-done.4), kind=kOutput, calls=%fused_computation.59 | convolution fusion | flops 402653184 | bytes 4390912 | tf_op jit(solution)/shard_map/dot_general | solution.py:55
  287.1 21.4 %all-to-all-done.2 = f32[2,256,512]{2,0,1:T(2,128)S(1)} async-done(((f32[2,256,512]{2,0,1:T(2,128)}), f32[2,256,512]{2,0,1:T(2,128)S(1)}, u32[]{:S(2)}, u32[]{:S(2)}) %all-to-all-start.2) | async-done | bytes 1048608 | tf_op jit(solution)/shard_map/all_to_all | solution.py:123
  310.9 1.8 gather_fusion
  312.6 1.8 bitcast_reduce_fusion
  (65 shorter events, 15.7 us)
Async XLA Ops:
  7.2 212.0 %copy-start = (bf16[2,2048,256]{2,1,0:T(8,128)(2,1)S(1)}, bf16[2,2048,256]{2,1,0:T(8,128)(2,1)}, u32[]{:S(2)}) copy-start(bf16[2,2048,256]{2,1,0:T(8,128)(2,1)} %param.22) | copy-start | bytes 6291460
  7.2 46.7 %all-gather.4.cloned.1.call-start = ((), (), s32[]{:S(2)}) async-start(), calls=%async_computation.5 | async-start | bytes 1179648 | tf_op jit(solution)/shard_map/all_gather | solution.py:39
  10.1 123.8 %reduce-scatter.3.cloned.1.call-start = ((), (), s32[]{:S(2)}) async-start(), calls=%async_computation.6 | async-start | bytes 2359296 | tf_op jit(solution)/shard_map/reduce_scatter | solution.py:58
  53.9 3.3 %copy-start.3 = (bf16[2048,384]{1,0:T(8,128)(2,1)S(1)}, bf16[2048,384]{1,0:T(8,128)(2,1)}, u32[]{:S(2)}) copy-start(bf16[2048,384]{1,0:T(8,128)(2,1)} %param.15) | copy-start | bytes 4718596
  56.5 0.7 copy-start.4
  57.2 2.1 copy-start.7
  59.2 1.4 copy-start.5
  64.4 70.6 %copy-start.8 = (f32[32,8]{0,1:T(8,128)S(1)}, f32[32,8]{0,1:T(8,128)}, u32[]{:S(2)}) copy-start(f32[32,8]{0,1:T(8,128)} %param.19) | copy-start | bytes 3076
  64.4 103.2 %copy-start.2 = (bf16[32,2048]{1,0:T(8,128)(2,1)S(1)}, bf16[32,2048]{1,0:T(8,128)(2,1)}, u32[]{:S(2)}) copy-start(bf16[32,2048]{1,0:T(8,128)(2,1)} %param.12) | copy-start | bytes 393220
  64.4 103.2 %copy-start.6 = (f32[2048]{0:T(1024)S(1)}, f32[2048]{0:T(1024)}, u32[]{:S(2)}) copy-start(f32[2048]{0:T(1024)} %param.14) | copy-start | bytes 24580
  66.4 67.6 %all-to-all-start.1 = ((bf16[16,32,512]{2,1,0:T(8,128)(2,1)}), bf16[16,32,512]{2,1,0:T(8,128)(2,1)S(1)}, u32[]{:S(2)}, u32[]{:S(2)}) async-start(bf16[16,32,512]{2,1,0:T(8,128)(2,1)} %constant_dynamic-slice_fusion), calls=%async_computation.2 | async-start | bytes 1048576 | tf_op jit(solution)/shard_map/all_to_all | solution.py:101
  69.9 97.7 %all-reduce.5.cloned.1.call-start = ((), (), s32[]{:S(2)}) async-start(), calls=%async_computation.7 | async-start | bytes 524288 | tf_op jit(solution)/shard_map/psum | solution.py:66
  134.0 60.5 %all-gather.8.cloned.1.call-start = ((), (), s32[]{:S(2)}) async-start(), calls=%async_computation.9 | async-start | bytes 2621440 | tf_op jit(solution)/shard_map/all_gather | solution.py:105
  134.9 81.3 %all-gather.6.cloned.1.call-start = ((), (), s32[]{:S(2)}) async-start(), calls=%async_computation.8 | async-start | bytes 2621440 | tf_op jit(solution)/shard_map/all_gather | solution.py:106
  194.2 80.0 %reduce-scatter.5.cloned.1.call-start = ((), (), s32[]{:S(2)}) async-start(), calls=%async_computation.10 | async-start | bytes 5242880 | tf_op jit(solution)/shard_map/reduce_scatter | solution.py:122
  277.3 31.2 %all-to-all-start.2 = ((f32[2,256,512]{2,0,1:T(2,128)}), f32[2,256,512]{2,0,1:T(2,128)S(1)}, u32[]{:S(2)}, u32[]{:S(2)}) async-start(f32[2,256,512]{2,0,1:T(2,128)} %copy.40), calls=%async_computation.4 | async-start | bytes 2097152 | tf_op jit(solution)/shard_map/all_to_all | solution.py:123
  308.4 1.0 copy-start.1
Sparse Core Ops, SparseCore 0:
  10.7 43.1 all-gather.3
  59.4 74.5 reduce-scatter.2
  136.3 31.2 all-reduce.4
  169.0 22.5 all-gather.7
  194.4 21.8 all-gather.5
  229.8 44.4 reduce-scatter.4
where the time goes:
time: 322 us; the launch traced here: 321 us
  waiting for transfers between devices  208 us (65%)
  blocking collectives  31.8 us (10%)
  matrix products  24.6 us (8%)
  local copies, waits for them, and re-layouts  20.8 us (6%)
  between operations  14.9 us (5%)
  other arithmetic  12.2 us (4%)
  starting transfers between devices  9.43 us (3%)
    reduce_scatter x1, waiting for transfers between devices, on_device(): lax.psum_scatter(lax.dot_general(score_grad, head_weight, (((1,), (1,)),...  64 us
    reduce_scatter x1, waiting for transfers between devices, on_device(): lax.psum_scatter(partial_input, 'vocab', scatter_dimension=2, tiled=True)  44.6 us
    psum x1, waiting for transfers between devices, on_device(): normed_grad = lax.psum(partial_grad, 'vocab')  32.5 us
    all_gather x1, waiting for transfers between devices, on_device(): lax.all_gather(normed, 'expert', axis=0, tiled=True)  26.3 us
    all_to_all x1, waiting for transfers between devices, on_device(): lax.all_to_all(slot_share, 'expert', split_axis=1, concat_axis=0, tiled=T...  21.4 us
    all_gather x1, waiting for transfers between devices, on_device(): lax.all_gather(moved_grads, 'vocab', axis=2, tiled=True)  18.8 us
    all_to_all x1, blocking collectives, on_device(): lax.all_to_all(part_grads, 'expert', split_axis=0, concat_axis=1, tiled=T...  18.6 us
    unnamed x1, blocking collectives  13.1 us
  transfers between devices with their start and end apart: 8, of which 6 were waited for; matrix products, arithmetic and copies ran while one was open for 8% of the time, Pallas kernels for 0%

commit v1 on v0

--- a/solution.py
+++ b/solution.py
@@ -63,7 +63,8 @@
         scatter_dimension=0,
         tiled=True,
     )
-    normed_grad = lax.psum(partial_grad, "vocab")
+    parts = lax.all_gather(partial_grad, "vocab", axis=0, tiled=False)
+    normed_grad = parts.sum(axis=0)
     gained = final_gain[None, :] * normed_grad
     residual_full = (
         gained - unit_rows * jnp.mean(unit_rows * gained, axis=1, keepdims=True)

time: 322 us -> 302 us (0.938)
  waiting for transfers between devices: 208 us -> 177 us
  blocking collectives: 31.8 us -> 46.9 us
  starting transfers between devices: 9.43 us -> 5.94 us
    psum x1 -> x0, waiting for transfers between devices: 32.5 us -> none  [on_device(): normed_grad = lax.psum(partial_grad, 'vocab')]
    all_to_all x0 -> x1, blocking collectives: none -> 16.5 us  [on_device(): lax.all_to_all(part_inputs, 'expert', split_axis=0, concat_axis=1, tiled=...]
    all_to_all x1 -> x0, starting transfers between devices: 3.49 us -> none  [on_device(): lax.all_to_all(part_inputs, 'expert', split_axis=0, concat_axis=1, tiled=...]
  transfers between devices with their start and end apart: 8 -> 7, of which waited for: 6 -> 5; matrix products, arithmetic and copies ran while one was open for 8% -> 8% of each run, Pallas kernels for 0% -> 0%
where the time goes in v1:
time: 302 us; the launch traced here: 301 us
  waiting for transfers between devices  177 us (59%)
  blocking collectives  46.9 us (16%)
  matrix products  24.6 us (8%)
  local copies, waits for them, and re-layouts  19.8 us (7%)
  between operations  15 us (5%)
  other arithmetic  11.6 us (4%)
  starting transfers between devices  5.94 us (2%)
    reduce_scatter x1, waiting for transfers between devices, on_device(): lax.psum_scatter(lax.dot_general(score_grad, head_weight, (((1,), (1,)),...  66.1 us
    reduce_scatter x1, waiting for transfers between devices, on_device(): lax.psum_scatter(partial_input, 'vocab', scatter_dimension=2, tiled=True)  44.6 us
    all_gather x1, waiting for transfers between devices, on_device(): lax.all_gather(normed, 'expert', axis=0, tiled=True)  26.3 us
    all_to_all x1, waiting for transfers between devices, on_device(): lax.all_to_all(slot_share, 'expert', split_axis=1, concat_axis=0, tiled=T...  21.4 us
    all_gather x1, waiting for transfers between devices, on_device(): lax.all_gather(moved_grads, 'vocab', axis=2, tiled=True)  18.6 us
    all_to_all x1, blocking collectives, on_device(): lax.all_to_all(part_grads, 'expert', split_axis=0, concat_axis=1, tiled=T...  17.3 us
    all_to_all x1, blocking collectives, on_device(): lax.all_to_all(part_inputs, 'expert', split_axis=0, concat_axis=1, tiled=...  16.5 us
    unnamed x1, blocking collectives  13.1 us
  transfers between devices with their start and end apart: 7, of which 5 were waited for; matrix products, arithmetic and copies ran while one was open for 8% of the time, Pallas kernels for 0%

profile of v1, /device:TPU:0, one launch (start us, length us, event | category | flops | bytes accessed | tf_op | source)
XLA Modules:
  0.0 300.9 jit_solution(13419283740276331426)
XLA Ops:
  8.4 1.7 multiply_convert_fusion.2
  13.8 13.1 %all-reduce.2 = (s32[256]{0:T(256)S(1)}, s32[256]{0:T(256)S(1)}) all-reduce(s32[256]{0:T(256)S(1)} %dynamic-update-slice.1, s32[256]{0:T(256)S(1)} %dynamic-update-slice), channel_id=1, replica_groups=mesh['expert'=8,'vocab'=4] {'expert'}, use_global_device_ids=true, to_apply=%add.1 | all-reduce | flops 512 | bytes 4096
  27.7 26.3 %all-gather.6.cloned.1.call-done = bf16[256,2048]{1,0:T(8,128)(2,1)} async-done(((bf16[32,2048]{1,0:T(8,128)(2,1)}), bf16[256,2048]{1,0:T(8,128)(2,1)}) %all-gather.6.cloned.1.call-update) | async-done | bytes 1048592 | tf_op jit(solution)/shard_map/all_gather | solution.py:39
  53.9 2.6 fusion.6
  57.2 2.1 fusion.30
  60.4 66.1 %reduce-scatter.3.cloned.1.call-done = f32[32,2048]{1,0:T(8,128)} async-done(((f32[256,2048]{1,0:T(8,128)}), f32[32,2048]{1,0:T(8,128)}) %reduce-scatter.3.cloned.1.call-update) | async-done | bytes 262160 | tf_op jit(solution)/shard_map/reduce_scatter | solution.py:58
  126.9 3.7 %scatter_custom_fusion.1 = bf16[512,2048]{1,0:T(8,128)(2,1)} fusion(s32[256]{0:T(256)S(1)} %bitcast.70, bf16[]{:T(256)} %constant.39.clone.1, bf16[32,2048]{1,0:T(8,128)(2,1)S(1)} %copy-done.5), kind=kCustom, calls=%fused_computation.16 | custom fusion | bytes 2228226 | tf_op jit(solution)/shard_map/scatter | solution.py:90
  131.7 16.5 %all_to_all.51 = bf16[16,32,512]{2,1,0:T(8,128)(2,1)S(1)} all-to-all(bf16[16,32,512]{2,1,0:T(8,128)(2,1)S(1)} %constant_dynamic-slice_fusion), channel_id=1, replica_groups=mesh['expert'=8,'vocab'=4] {'expert'}, dimensions={0} | all-to-all | bytes 1048576 | tf_op jit(solution)/shard_map/all_to_all | solution.py:102
  149.3 1.3 reduce_sum.58
  151.0 3.8 %scatter_custom_fusion = bf16[512,2048]{1,0:T(8,128)(2,1)} fusion(s32[256]{0:T(256)S(1)} %bitcast.71, f32[32,2048]{1,0:T(8,128)S(1)} %subtract_divide_fusion, f32[256]{0:T(256)S(1)} %mul.124, bf16[]{:T(256)} %constant.39.clone.1), kind=kCustom, calls=%fused_computation.15 | custom fusion | flops 1048576 | bytes 2360322 | tf_op jit(solution)/shard_map/scatter | solution.py:96
  155.9 17.3 %all_to_all.52 = bf16[16,32,512]{2,1,0:T(8,128)(2,1)S(1)} all-to-all(bf16[16,32,512]{2,1,0:T(8,128)(2,1)S(1)} %constant_dynamic-slice_fusion.1), channel_id=1, replica_groups=mesh['expert'=8,'vocab'=4] {'expert'}, dimensions={0} | all-to-all | bytes 1048576 | tf_op jit(solution)/shard_map/all_to_all | solution.py:103
  174.3 2.9 fusion.32
  177.3 18.6 %all-gather.8.cloned.1.call-done = bf16[2,256,2048]{2,1,0:T(8,128)(2,1)} async-done(((bf16[2,256,512]{2,1,0:T(8,128)(2,1)}), bf16[2,256,2048]{2,1,0:T(8,128)(2,1)}) %all-gather.8.cloned.1.call-update) | async-done | bytes 2097168 | tf_op jit(solution)/shard_map/all_gather | solution.py:107
  195.8 3.0 fusion.31
  198.8 5.6 %fusion.7 = f32[2,256,2048]{2,1,0:T(8,128)} fusion(bf16[2,2048,256]{2,1,0:T(8,128)(2,1)} %param.21, f32[2,256,256]{2,1,0:T(8,128)S(1)} %fusion.31, bf16[2,256,2048]{2,1,0:T(8,128)(2,1)} %all-gather.10.cloned.1.call-done, bf16[2,2048,256]{2,1,0:T(8,128)(2,1)S(1)} %copy-done, f32[2,256,256]{2,1,0:T(8,128)S(1)} %fusion.32), kind=kOutput, calls=%fused_computation.14 | convolution fusion | flops 1075052544 | bytes 11534336 | tf_op jit(solution)/shard_map/esf,edf->esd/dot_general | solution.py:117
  204.4 4.9 %convolution_add_fusion = f32[2,256,2048]{2,1,0:T(8,128)} fusion(f32[2,256,2048]{2,1,0:T(8,128)} %fusion.7, bf16[2,2048,256]{2,1,0:T(8,128)(2,1)S(1)} %copy-done, f32[2,256,256]{2,1,0:T(8,128)S(1)} %fusion.31, f32[2,256,256]{2,1,0:T(8,128)S(1)} %fusion.32), kind=kOutput, calls=%fused_computation.3 | convolution fusion | flops 538705920 | bytes 11534336 | tf_op jit(solution)/shard_map/esf,edf->esd/dot_general | solution.py:120
  209.3 44.6 %reduce-scatter.5.cloned.1.call-done = f32[2,256,512]{2,1,0:T(8,128)} async-done(((f32[2,256,2048]{2,1,0:T(8,128)}), f32[2,256,512]{2,1,0:T(8,128)}) %reduce-scatter.5.cloned.1.call-update) | async-done | bytes 1048592 | tf_op jit(solution)/shard_map/reduce_scatter | solution.py:123
  253.9 3.0 %copy.40 = f32[2,256,512]{2,0,1:T(2,128)} copy(f32[2,256,512]{2,1,0:T(8,128)} %reduce-scatter.5.cloned.1.call-done) | data formatting | bytes 2097152 | tf_op jit(solution)/shard_map/reduce_scatter | solution.py:123
  256.9 5.5 %all-to-all-start.2 = ((f32[2,256,512]{2,0,1:T(2,128)}), f32[2,256,512]{2,0,1:T(2,128)S(1)}, u32[]{:S(2)}, u32[]{:S(2)}) async-start(f32[2,256,512]{2,0,1:T(2,128)} %copy.40), calls=%async_computation.4 | async-start | bytes 2097152 | tf_op jit(solution)/shard_map/all_to_all | solution.py:124
  262.4 3.7 %fusion.29 = f32[2048,384]{1,0:T(8,128)} fusion(bf16[256,2048]{1,0:T(8,128)(2,1)} %all-gather.6.cloned.1.call-done, bf16[256,384]{1,0:T(8,128)(2,1)} %copy-done.4), kind=kOutput, calls=%fused_computation.59 | convolution fusion | flops 402653184 | bytes 4390912 | tf_op jit(solution)/shard_map/dot_general | solution.py:55
  266.7 21.4 %all-to-all-done.2 = f32[2,256,512]{2,0,1:T(2,128)S(1)} async-done(((f32[2,256,512]{2,0,1:T(2,128)}), f32[2,256,512]{2,0,1:T(2,128)S(1)}, u32[]{:S(2)}, u32[]{:S(2)}) %all-to-all-start.2) | async-done | bytes 1048608 | tf_op jit(solution)/shard_map/all_to_all | solution.py:124
  289.1 1.4 copy.41
  290.5 1.8 gather_fusion
  292.2 1.8 bitcast_reduce_fusion
  (65 shorter events, 13.5 us)
Async XLA Ops:
  7.2 191.6 %copy-start = (bf16[2,2048,256]{2,1,0:T(8,128)(2,1)S(1)}, bf16[2,2048,256]{2,1,0:T(8,128)(2,1)}, u32[]{:S(2)}) copy-start(bf16[2,2048,256]{2,1,0:T(8,128)(2,1)} %param.22) | copy-start | bytes 6291460
  7.2 46.7 %all-gather.6.cloned.1.call-start = ((), (), s32[]{:S(2)}) async-start(), calls=%async_computation.5 | async-start | bytes 1179648 | tf_op jit(solution)/shard_map/all_gather | solution.py:39
  10.1 116.4 %reduce-scatter.3.cloned.1.call-start = ((), (), s32[]{:S(2)}) async-start(), calls=%async_computation.6 | async-start | bytes 2359296 | tf_op jit(solution)/shard_map/reduce_scatter | solution.py:58
  53.9 3.3 %copy-start.3 = (bf16[2048,384]{1,0:T(8,128)(2,1)S(1)}, bf16[2048,384]{1,0:T(8,128)(2,1)}, u32[]{:S(2)}) copy-start(bf16[2048,384]{1,0:T(8,128)(2,1)} %param.15) | copy-start | bytes 4718596
  56.5 0.7 copy-start.4
  57.2 2.1 copy-start.7
  59.2 67.6 %copy-start.5 = (bf16[32,2048]{1,0:T(8,128)(2,1)S(1)}, bf16[32,2048]{1,0:T(8,128)(2,1)}, u32[]{:S(2)}) copy-start(bf16[32,2048]{1,0:T(8,128)(2,1)} %param.13) | copy-start | bytes 393220
  59.3 90.0 %all-gather.12.cloned.1.call-start = ((), (), s32[]{:S(2)}) async-start(), calls=%async_computation.10 | async-start | bytes 1310720 | tf_op jit(solution)/shard_map/all_gather | solution.py:66
  126.6 47.7 %all-gather.10.cloned.1.call-start = ((), (), s32[]{:S(2)}) async-start(), calls=%async_computation.8 | async-start | bytes 2621440 | tf_op jit(solution)/shard_map/all_gather | solution.py:106
  130.6 18.5 %copy-start.8 = (f32[32,8]{0,1:T(8,128)S(1)}, f32[32,8]{0,1:T(8,128)}, u32[]{:S(2)}) copy-start(f32[32,8]{0,1:T(8,128)} %param.19) | copy-start | bytes 3076
  131.7 18.9 %copy-start.2 = (bf16[32,2048]{1,0:T(8,128)(2,1)S(1)}, bf16[32,2048]{1,0:T(8,128)(2,1)}, u32[]{:S(2)}) copy-start(bf16[32,2048]{1,0:T(8,128)(2,1)} %param.12) | copy-start | bytes 393220
  131.7 18.9 %copy-start.6 = (f32[2048]{0:T(1024)S(1)}, f32[2048]{0:T(1024)}, u32[]{:S(2)}) copy-start(f32[2048]{0:T(1024)} %param.14) | copy-start | bytes 24580
  149.1 46.8 %all-gather.8.cloned.1.call-start = ((), (), s32[]{:S(2)}) async-start(), calls=%async_computation.7 | async-start | bytes 2621440 | tf_op jit(solution)/shard_map/all_gather | solution.py:107
  174.1 79.8 %reduce-scatter.5.cloned.1.call-start = ((), (), s32[]{:S(2)}) async-start(), calls=%async_computation.9 | async-start | bytes 5242880 | tf_op jit(solution)/shard_map/reduce_scatter | solution.py:123
  256.9 31.2 %all-to-all-start.2 = ((f32[2,256,512]{2,0,1:T(2,128)}), f32[2,256,512]{2,0,1:T(2,128)S(1)}, u32[]{:S(2)}, u32[]{:S(2)}) async-start(f32[2,256,512]{2,0,1:T(2,128)} %copy.40), calls=%async_computation.4 | async-start | bytes 2097152 | tf_op jit(solution)/shard_map/all_to_all | solution.py:124
  288.1 1.0 copy-start.1
Sparse Core Ops, SparseCore 0:
  10.7 43.1 all-gather.5
  59.4 67.1 reduce-scatter.2
  128.1 15.6 all-gather.11
  149.2 21.6 all-gather.9
  174.2 21.6 all-gather.7
  209.4 44.4 reduce-scatter.4
